TPU v7x, 32 devices: a whole 2x2x4 slice. The times are simulated.
32 devices in a mesh: seq: 8 (over z, x), head: 4 (over y, core).
Axes of the slice: x: 2, y: 2, z: 4, core: 2. Of those that a mesh axis runs over, the one named last changes fastest.
Arguments:
- q_latent: bfloat16 [2048, 1536], P('seq', 'head'), may hold values from -6 to 6
- kv_latent: bfloat16 [2048, 512], P('seq', 'head'), may hold values from -6 to 6
- k_rope: bfloat16 [2048, 64], P('seq'), may hold values from -6 to 6
- segment_ids: int32 [2048], P('seq'), may hold values from 0 to 7, as said below
- w_q_nope: bfloat16 [1536, 16384], P('seq', 'head'), may hold values from -6 to 6
- w_q_rope: bfloat16 [1536, 8192], P('seq', 'head'), may hold values from -6 to 6
- w_kv_nope: bfloat16 [512, 16384], P('seq', 'head'), may hold values from -6 to 6
- threshold: float32 [1], replicated, may hold values from 3.5 to 5.5
Outputs:
- new_q_nope: bfloat16 [1536, 16384], P('seq', 'head')
- new_q_rope: bfloat16 [1536, 8192], P('seq', 'head')
- new_kv_nope: bfloat16 [512, 16384], P('seq', 'head')
- head_max: float32 [128], P('head')
- row_max: float32 [2048, 128], P('seq', 'head')
Inputs may be any that keep to these rules, and one draw needn't show every extreme that they name: segment_ids never fall along the tokens and each document has 1 to 768 tokens.
All inputs are finite; a program needn't handle non-finite values.
Results may differ from a plain program's by a relative error of at most 0.0034.
Values may be sent and summed in bfloat16 or wider, within the bound.
A program may use at most 128 MiB of HBM per device.

v0:
```python
import math

import jax
import jax.numpy as jnp
from jax import lax
from jax.sharding import PartitionSpec as P

D_NOPE = 128
D_ROPE = 64
QLORA = 1536
KVLORA = 512
REACH = 3


def as_sent(value):
    return jax.tree.map(lambda a: a.astype(jnp.bfloat16) if a.dtype == jnp.float32 else a, value)


def from_partner(value, axis, stride):
    mask = 2**stride
    pairs = [(source, source ^ mask) for source in range(lax.axis_size(axis))]
    return lax.ppermute(value, axis, pairs)


def shifted(block, axis, distance):
    devices = range(lax.axis_size(axis))
    route = [(i - distance, i) for i in devices if i - distance in devices]
    return lax.ppermute(block, axis, route)


def score_max(query_nope, query_rope, key_nope, key_rope, allowed):
    nope = jnp.einsum("qhd,khd->hqk", query_nope, key_nope, preferred_element_type=jnp.float32)
    rope = jnp.einsum("qhd,kd->hqk", query_rope, key_rope, preferred_element_type=jnp.float32)
    scores = (nope + rope) * (1.0 / math.sqrt(D_NOPE + D_ROPE))
    return jnp.max(jnp.where(allowed[None], scores, jnp.float32(-1e30)), axis=2)


def masked_max(compute, operands):
    return compute(*operands)


def spread_columns(weight, width, quarter, copies):
    pieces = weight.reshape(weight.shape[0], 4, quarter * width).transpose(1, 0, 2)
    return jnp.tile(pieces, (copies, 1, 1))


def body(q_latent, kv_latent, k_rope, segment_ids, w_q_nope, w_q_rope, w_kv_nope, threshold):
    q_whole, kv_whole = (
        lax.all_gather(q_latent, "head", axis=1, tiled=True),
        lax.all_gather(kv_latent, "head", axis=1, tiled=True),
    )
    rows = q_whole.shape[0]
    heads = w_q_nope.shape[1] // D_NOPE
    q_scale = 1.0 / math.sqrt(QLORA)
    k_scale = 1.0 / math.sqrt(KVLORA)
    place = lax.axis_index("seq")
    quarter = heads // 4
    copies = lax.axis_size("seq") // 4
    slot = place % 4
    sent = (
        spread_columns(w_q_nope, D_NOPE, quarter, copies),
        spread_columns(w_q_rope, D_ROPE, quarter, copies),
        spread_columns(w_kv_nope, D_NOPE, quarter, copies),
    )
    got_nope, got_rope, got_kv = (
        lax.all_to_all(sent[0], "seq", split_axis=0, concat_axis=1, tiled=True),
        lax.all_to_all(sent[1], "seq", split_axis=0, concat_axis=1, tiled=True),
        lax.all_to_all(sent[2], "seq", split_axis=0, concat_axis=1, tiled=True),
    )
    sub_nope = got_nope.reshape(QLORA, quarter * D_NOPE)
    sub_rope = got_rope.reshape(QLORA, quarter * D_ROPE)
    sub_kv = got_kv.reshape(KVLORA, quarter * D_NOPE)
    group = (q_whole, kv_whole, k_rope)
    for level in range(2):
        partner = jax.tree.map(
            lambda part, own: part.astype(own.dtype),
            from_partner(as_sent(group), "seq", level),
            group,
        )
        upper = place // (1 << level) % 2 == 1
        group = tuple(
            (
                jnp.where(
                    upper, jnp.concatenate([other, mine], 0), jnp.concatenate([mine, other], 0)
                )
                for mine, other in zip(group, partner)
            )
        )
    group_q, group_kv, group_rope = group
    early_kv, early_rope = shifted(
        (group_kv[(4 - REACH) * rows :], group_rope[(4 - REACH) * rows :]), "seq", 4
    )
    keys_kv = jnp.concatenate([early_kv, group_kv], 0)
    keys_rope = jnp.concatenate([early_rope, group_rope], 0)
    key_nope = (
        (jnp.dot(keys_kv, sub_kv, preferred_element_type=jnp.float32) * k_scale)
        .astype(jnp.bfloat16)
        .reshape(keys_kv.shape[0], quarter, D_NOPE)
    )
    query_nope = (
        (jnp.dot(group_q, sub_nope, preferred_element_type=jnp.float32) * q_scale)
        .astype(jnp.bfloat16)
        .reshape(4 * rows, quarter, D_NOPE)
    )
    query_rope = (
        (jnp.dot(group_q, sub_rope, preferred_element_type=jnp.float32) * q_scale)
        .astype(jnp.bfloat16)
        .reshape(4 * rows, quarter, D_ROPE)
    )
    all_segs = lax.all_gather(segment_ids, "seq", axis=0, tiled=True)
    padded_segs = jnp.concatenate([jnp.full((REACH * rows,), -1, jnp.int32), all_segs], 0)
    first = place // 4 * 4
    window = (REACH + 1) * rows
    block_rows = []
    for local in range(4):
        block = first + local
        query_seg = lax.dynamic_slice_in_dim(all_segs, block * rows, rows, 0)
        key_seg = lax.dynamic_slice_in_dim(padded_segs, block * rows, window, 0)
        query_pos = block * rows + jnp.arange(rows, dtype=jnp.int32)
        key_pos = (block - REACH) * rows + jnp.arange(window, dtype=jnp.int32)
        allowed = (
            (query_seg[:, None] == key_seg[None, :])
            & (key_pos[None, :] <= query_pos[:, None])
            & (key_pos[None, :] >= 0)
        )
        operands = (
            query_nope[local * rows : (local + 1) * rows],
            query_rope[local * rows : (local + 1) * rows],
            key_nope[local * rows : local * rows + window],
            keys_rope[local * rows : local * rows + window],
            allowed,
        )
        block_rows.append(masked_max(score_max, operands))
    stacked = jnp.stack(block_rows, 0)[None]
    for level in range(2):
        partner = from_partner(stacked, "seq", level)
        upper = place // (1 << level) % 2 == 1
        stacked = jnp.where(
            upper, jnp.concatenate([partner, stacked], 0), jnp.concatenate([stacked, partner], 0)
        )
    own = lax.dynamic_index_in_dim(stacked, slot, 1, False)
    row_max = own.reshape(heads, rows).T
    local_heads = jnp.max(row_max, axis=0)
    head_max = lax.pmax(local_heads, "seq")
    clip = threshold[0] / jnp.maximum(head_max, threshold[0])
    root = jnp.sqrt(clip)
    new_q_nope = (w_q_nope.astype(jnp.float32) * jnp.repeat(root, D_NOPE)[None, :]).astype(
        jnp.bfloat16
    )
    new_q_rope = (w_q_rope.astype(jnp.float32) * jnp.repeat(clip, D_ROPE)[None, :]).astype(
        jnp.bfloat16
    )
    new_kv_nope = (w_kv_nope.astype(jnp.float32) * jnp.repeat(root, D_NOPE)[None, :]).astype(
        jnp.bfloat16
    )
    return (new_q_nope, new_q_rope, new_kv_nope, head_max, row_max)


def solution(mesh):
    in_specs = (
        P("seq", "head"),
        P("seq", "head"),
        P("seq", None),
        P("seq"),
        P("seq", "head"),
        P("seq", "head"),
        P("seq", "head"),
        P(),
    )
    out_specs = (P("seq", "head"), P("seq", "head"), P("seq", "head"), P("head"), P("seq", "head"))
    return jax.shard_map(body, mesh=mesh, in_specs=in_specs, out_specs=out_specs, check_vma=False)
```

profile of v0, /device:TPU:0, one launch (start us, length us, event | category | flops | bytes accessed | tf_op | source)
XLA Modules:
  0.0 299.3 jit_solution(7385676597361516628)
XLA Ops:
  0.6 1.5 reshape.406
  3.4 7.3 %all-to-all-start.1 = ((bf16[8,64,1024]{2,1,0:T(8,128)(2,1)}), bf16[8,64,1024]{2,1,0:T(8,128)(2,1)S(1)}, u32[]{:S(2)}, u32[]{:S(2)}) async-start(bf16[8,64,1024]{2,1,0:T(8,128)(2,1)} %bitcast.8), calls=%async_computation.1 | async-start | bytes 2097152 | tf_op jit(solution)/shard_map/all_to_all | solution.py:68
  11.4 25.0 %all-to-all-done.1 = bf16[8,64,1024]{2,1,0:T(8,128)(2,1)S(1)} async-done(((bf16[8,64,1024]{2,1,0:T(8,128)(2,1)}), bf16[8,64,1024]{2,1,0:T(8,128)(2,1)S(1)}, u32[]{:S(2)}, u32[]{:S(2)}) %all-to-all-start.1) | async-done | bytes 1048608 | tf_op jit(solution)/shard_map/all_to_all | solution.py:68
  37.9 4.3 %all-to-all-start.2 = ((bf16[8,192,512]{2,1,0:T(8,128)(2,1)}), bf16[8,192,512]{2,1,0:T(8,128)(2,1)}, u32[]{:S(2)}, u32[]{:S(2)}) async-start(bf16[8,192,512]{2,1,0:T(8,128)(2,1)} %bitcast.13), calls=%async_computation.2 | async-start | bytes 3145728 | tf_op jit(solution)/shard_map/all_to_all | solution.py:67
  43.9 34.9 %all-to-all-done.2 = bf16[8,192,512]{2,1,0:T(8,128)(2,1)} async-done(((bf16[8,192,512]{2,1,0:T(8,128)(2,1)}), bf16[8,192,512]{2,1,0:T(8,128)(2,1)}, u32[]{:S(2)}, u32[]{:S(2)}) %all-to-all-start.2) | async-done | bytes 1572896 | tf_op jit(solution)/shard_map/all_to_all | solution.py:67
  78.8 2.1 tile.12
  81.0 4.6 %all-to-all-start = ((bf16[8,192,1024]{2,1,0:T(8,128)(2,1)}), bf16[8,192,1024]{2,1,0:T(8,128)(2,1)}, u32[]{:S(2)}, u32[]{:S(2)}) async-start(bf16[8,192,1024]{2,1,0:T(8,128)(2,1)} %bitcast.4), calls=%async_computation | async-start | bytes 6291456 | tf_op jit(solution)/shard_map/all_to_all | solution.py:66
  85.6 1.9 collective-permute-start.5
  87.5 5.8 %all_gather.11 = bf16[256,512]{1,0:T(8,128)(2,1)S(1)} all-gather(bf16[256,128]{1,0:T(8,128)(2,1)S(1)} %copy-done.15), channel_id=1, replica_groups=mesh['seq'=8,'head'=4] {'head'}, dimensions={1}, use_global_device_ids=true | all-gather | bytes 327680 | tf_op jit(solution)/shard_map/all_gather | solution.py:50
  93.5 8.6 %all_gather.10 = bf16[256,1536]{1,0:T(8,128)(2,1)S(1)} all-gather(bf16[256,384]{1,0:T(8,128)(2,1)S(1)} %copy-done.14), channel_id=1, replica_groups=mesh['seq'=8,'head'=4] {'head'}, dimensions={1}, use_global_device_ids=true | all-gather | bytes 983040 | tf_op jit(solution)/shard_map/all_gather | solution.py:49
  102.1 1.8 collective-permute-start
  104.0 50.2 %all-gather = s32[8,1,256]{2,1,0:T(1,128)S(1)} all-gather(s32[1,1,256]{2,1,0:T(1,128)S(1)} %bitcast.118), channel_id=1, replica_groups=mesh['seq'=8,'head'=4] {'seq'}, dimensions={0}, use_global_device_ids=true | all-gather | bytes 9216 | tf_op jit(solution)/shard_map/all_gather | solution.py:110
  154.6 11.1 %collective-permute-start.3 = (bf16[512,512]{1,0:T(8,128)(2,1)S(1)}, bf16[512,512]{1,0:T(8,128)(2,1)S(1)}, u32[]{:S(2)}, u32[]{:S(2)}) collective-permute-start(bf16[512,512]{1,0:T(8,128)(2,1)S(1)} %maximum_select_fusion.5), channel_id=1, source_target_pairs={{0,8},{4,12},{8,0},{12,4},{16,24},{20,28},{24,16},{28,20},{1,9},{5... | collective-permute-start | bytes 1572872 | tf_op jit(solution)/shard_map/ppermute | solution.py:22
  167.3 6.2 %collective-permute-done.3 = bf16[512,512]{1,0:T(8,128)(2,1)S(1)} collective-permute-done((bf16[512,512]{1,0:T(8,128)(2,1)S(1)}, bf16[512,512]{1,0:T(8,128)(2,1)S(1)}, u32[]{:S(2)}, u32[]{:S(2)}) %collective-permute-start.3) | collective-permute-done | bytes 524320 | tf_op jit(solution)/shard_map/ppermute | solution.py:22
  174.1 4.7 %collective-permute-start.4 = (bf16[768,512]{1,0:T(8,128)(2,1)S(1)}, bf16[768,512]{1,0:T(8,128)(2,1)S(1)}, u32[]{:S(2)}, u32[]{:S(2)}) collective-permute-start(bf16[768,512]{1,0:T(8,128)(2,1)S(1)} %slice.117), channel_id=1, source_target_pairs={{0,16},{4,20},{8,24},{12,28},{1,17},{5,21},{9,25},{13,29},{2,18},{... | collective-permute-start | bytes 2359304 | tf_op jit(solution)/shard_map/ppermute | solution.py:28
  180.1 1.5 collective-permute-start.6
  182.0 44.8 %collective-permute-done.6 = bf16[512,64]{0,1:T(8,128)(2,1)S(1)} collective-permute-done((bf16[512,64]{0,1:T(8,128)(2,1)S(1)}, bf16[512,64]{0,1:T(8,128)(2,1)S(1)}, u32[]{:S(2)}, u32[]{:S(2)}) %collective-permute-start.6) | collective-permute-done | bytes 65568 | tf_op jit(solution)/shard_map/ppermute | solution.py:22
  227.4 2.1 collective-permute-start.7
  229.6 2.2 multiply_convert_fusion
  231.8 3.0 fusion.37
  234.7 3.9 %multiply_convert_fusion.3 = bf16[1024,512]{0,1:T(8,128)(2,1)S(1)} fusion(bf16[1536,512]{1,0:T(8,128)(2,1)} %bitcast.14, bf16[512,1536]{1,0:T(8,128)(2,1)S(1)} %maximum_select_fusion.1, bf16[512,1536]{1,0:T(8,128)(2,1)S(1)} %collective-permute-done.1, pred[]{:T(512)S(6)} %eq.82), kind=kOutput, calls=%fused_computation.20 | convolution fusion | flops 1625817088 | bytes 5767169 | tf_op jit(solution)/shard_map/dot_general | solution.py:106
  239.5 7.3 %multiply_convert_fusion.1 = bf16[1024,1024]{0,1:T(8,128)(2,1)S(1)} fusion(bf16[1536,1024]{1,0:T(8,128)(2,1)} %bitcast.5, bf16[512,1536]{1,0:T(8,128)(2,1)} %copy-done.8, bf16[512,1536]{1,0:T(8,128)(2,1)} %copy-done.19, pred[]{:T(512)S(6)} %eq.82), kind=kOutput, calls=%fused_computation.17 | convolution fusion | flops 3237478400 | bytes 8388609 | tf_op jit(solution)/shard_map/dot_general | solution.py:101
  252.9 2.1 fusion.2
  255.0 1.5 fusion.42
  256.5 3.0 %fusion.11 = f32[8,256]{1,0:T(8,128)S(1)} fusion(f32[8,256,1024]{2,1,0:T(8,128)S(1)} %fusion.41, pred[256,1024]{1,0:T(8,128)(4,1)S(1)} %and_and_fusion.3, bf16[256,8,64]{0,2,1:T(8,128)(2,1)S(1)} %bitcast.109, bf16[1024,64]{0,1:T(8,128)(2,1)S(1)} %maximum_select_fusion.6, bf16[768,64]{0,1:T(8,128)(2,1)} %collective-permute-done.7), kind=kOutput, calls=%fused_computation.15 | convolution fusion | flops 277084160 | bytes 9150464 | tf_op jit(solution)/shard_map/qhd,kd->hqk/dot_general | solution.py:33
  259.6 2.9 fusion.5
  262.5 3.1 %fusion.8 = f32[8,256]{1,0:T(8,128)S(1)} fusion(f32[8,256,1024]{2,1,0:T(8,128)S(1)} %fusion.42, pred[256,1024]{1,0:T(8,128)(4,1)S(1)} %get-tuple-element.30, bf16[256,8,64]{0,2,1:T(8,128)(2,1)S(1)} %bitcast.107, bf16[1024,64]{0,1:T(8,128)(2,1)S(1)} %maximum_select_fusion.6, bf16[768,64]{0,1:T(8,128)(2,1)} %collective-permute-done.7), kind=kOutput, calls=%fused_computation.11 | convolution fusion | flops 277084160 | bytes 9150464 | tf_op jit(solution)/shard_map/qhd,kd->hqk/dot_general | solution.py:33
  265.7 3.4 %collective-permute-start.8 = (f32[1,4,8,256]{3,2,0,1:T(8,128)S(1)}, f32[1,4,8,256]{3,2,0,1:T(8,128)S(1)}, u32[]{:S(2)}, u32[]{:S(2)}) collective-permute-start(f32[1,4,8,256]{3,2,0,1:T(8,128)S(1)} %maximum_bitcast_fusion), channel_id=1, source_target_pairs={{0,4},{4,0},{8,12},{12,8},{16,20},{20,16},{24,28},{28,24},{1,5},{5... | collective-permute-start | bytes 98312 | tf_op jit(solution)/shard_map/ppermute | solution.py:22
  269.1 1.9 collective-permute-done.8
  271.0 2.5 collective-permute-start.9
  274.2 1.6 collective-permute-done.9
  276.5 19.1 %pmax.7 = f32[32]{0:T(128)S(1)} all-reduce(f32[32]{0:T(128)S(1)} %reduce_max.52), channel_id=1, replica_groups=mesh['seq'=8,'head'=4] {'seq'}, use_global_device_ids=true, to_apply=%region_5.6 | all-reduce | flops 32 | bytes 256 | tf_op jit(solution)/shard_map/pmax | solution.py:144
  (96 shorter events, 21.3 us)
Async XLA Ops:
  0.6 10.1 %copy-start.5 = (bf16[192,2048]{1,0:T(8,128)(2,1)S(1)}, bf16[192,2048]{1,0:T(8,128)(2,1)}, u32[]{:S(2)}) copy-start(bf16[192,2048]{1,0:T(8,128)(2,1)} %param.13) | copy-start | bytes 2359300
  3.4 33.0 %all-to-all-start.1 = ((bf16[8,64,1024]{2,1,0:T(8,128)(2,1)}), bf16[8,64,1024]{2,1,0:T(8,128)(2,1)S(1)}, u32[]{:S(2)}, u32[]{:S(2)}) async-start(bf16[8,64,1024]{2,1,0:T(8,128)(2,1)} %bitcast.8), calls=%async_computation.1 | async-start | bytes 2097152 | tf_op jit(solution)/shard_map/all_to_all | solution.py:68
  11.4 30.8 %copy-start.3 = (bf16[192,4096]{1,0:T(8,128)(2,1)S(1)}, bf16[192,4096]{1,0:T(8,128)(2,1)}, u32[]{:S(2)}) copy-start(bf16[192,4096]{1,0:T(8,128)(2,1)} %param.12) | copy-start | bytes 4718596
  36.5 1.5 copy-start.9
  37.9 40.9 %all-to-all-start.2 = ((bf16[8,192,512]{2,1,0:T(8,128)(2,1)}), bf16[8,192,512]{2,1,0:T(8,128)(2,1)}, u32[]{:S(2)}, u32[]{:S(2)}) async-start(bf16[8,192,512]{2,1,0:T(8,128)(2,1)} %bitcast.13), calls=%async_computation.2 | async-start | bytes 3145728 | tf_op jit(solution)/shard_map/all_to_all | solution.py:67
  80.9 4.6 %copy-start.16 = (bf16[256,64]{0,1:T(8,128)(2,1)S(1)}, bf16[256,64]{0,1:T(8,128)(2,1)}, u32[]{:S(2)}) copy-start(bf16[256,64]{0,1:T(8,128)(2,1)} %param.10) | copy-start | bytes 98308
  80.9 6.5 %copy-start.15 = (bf16[256,128]{1,0:T(8,128)(2,1)S(1)}, bf16[256,128]{1,0:T(8,128)(2,1)}, u32[]{:S(2)}) copy-start(bf16[256,128]{1,0:T(8,128)(2,1)} %param.9) | copy-start | bytes 196612
  80.9 12.5 %copy-start.14 = (bf16[256,384]{1,0:T(8,128)(2,1)S(1)}, bf16[256,384]{1,0:T(8,128)(2,1)}, u32[]{:S(2)}) copy-start(bf16[256,384]{1,0:T(8,128)(2,1)} %param.8) | copy-start | bytes 589828
  81.0 23.1 %copy-start.17 = (s32[256]{0:T(256)S(1)}, s32[256]{0:T(256)}, u32[]{:S(2)}) copy-start(s32[256]{0:T(256)} %param.11) | copy-start | bytes 3076
  81.0 158.5 %all-to-all-start = ((bf16[8,192,1024]{2,1,0:T(8,128)(2,1)}), bf16[8,192,1024]{2,1,0:T(8,128)(2,1)}, u32[]{:S(2)}, u32[]{:S(2)}) async-start(bf16[8,192,1024]{2,1,0:T(8,128)(2,1)} %bitcast.4), calls=%async_computation | async-start | bytes 6291456 | tf_op jit(solution)/shard_map/all_to_all | solution.py:66
  85.6 94.5 %collective-permute-start.5 = (bf16[256,64]{0,1:T(8,128)(2,1)S(1)}, bf16[256,64]{0,1:T(8,128)(2,1)S(1)}, u32[]{:S(2)}, u32[]{:S(2)}) collective-permute-start(bf16[256,64]{0,1:T(8,128)(2,1)S(1)} %copy-done.16), channel_id=1, source_target_pairs={{0,4},{4,0},{8,12},{12,8},{16,20},{20,16},{24,28},{28,24},{1,5},{5... | collective-permute-start | bytes 98312 | tf_op jit(solution)/shard_map/ppermute | solution.py:22
  93.3 61.1 %collective-permute-start.2 = (bf16[256,512]{1,0:T(8,128)(2,1)S(1)}, bf16[256,512]{1,0:T(8,128)(2,1)S(1)}, u32[]{:S(2)}, u32[]{:S(2)}) collective-permute-start(bf16[256,512]{1,0:T(8,128)(2,1)S(1)} %all_gather.11), channel_id=1, source_target_pairs={{0,4},{4,0},{8,12},{12,8},{16,20},{20,16},{24,28},{28,24},{1,5},{5... | collective-permute-start | bytes 786440 | tf_op jit(solution)/shard_map/ppermute | solution.py:22
  102.1 76.7 %collective-permute-start = (bf16[256,1536]{1,0:T(8,128)(2,1)S(1)}, bf16[256,1536]{1,0:T(8,128)(2,1)S(1)}, u32[]{:S(2)}, u32[]{:S(2)}) collective-permute-start(bf16[256,1536]{1,0:T(8,128)(2,1)S(1)} %all_gather.10), channel_id=1, source_target_pairs={{0,4},{4,0},{8,12},{12,8},{16,20},{20,16},{24,28},{28,24},{1,5},{5... | collective-permute-start | bytes 2359304 | tf_op jit(solution)/shard_map/ppermute | solution.py:22
  154.6 18.9 %collective-permute-start.3 = (bf16[512,512]{1,0:T(8,128)(2,1)S(1)}, bf16[512,512]{1,0:T(8,128)(2,1)S(1)}, u32[]{:S(2)}, u32[]{:S(2)}) collective-permute-start(bf16[512,512]{1,0:T(8,128)(2,1)S(1)} %maximum_select_fusion.5), channel_id=1, source_target_pairs={{0,8},{4,12},{8,0},{12,4},{16,24},{20,28},{24,16},{28,20},{1,9},{5... | collective-permute-start | bytes 1572872 | tf_op jit(solution)/shard_map/ppermute | solution.py:22
  174.0 55.6 %copy-start.10 = (bf16[8,64,1024]{2,1,0:T(8,128)(2,1)S(1)}, bf16[8,64,1024]{2,1,0:T(8,128)(2,1)}, u32[]{:S(2)}) copy-start(bf16[8,64,1024]{2,1,0:T(8,128)(2,1)} %copy-done.9) | copy-start | bytes 3145732
  174.1 55.5 %collective-permute-start.4 = (bf16[768,512]{1,0:T(8,128)(2,1)S(1)}, bf16[768,512]{1,0:T(8,128)(2,1)S(1)}, u32[]{:S(2)}, u32[]{:S(2)}) collective-permute-start(bf16[768,512]{1,0:T(8,128)(2,1)S(1)} %slice.117), channel_id=1, source_target_pairs={{0,16},{4,20},{8,24},{12,28},{1,17},{5,21},{9,25},{13,29},{2,18},{... | collective-permute-start | bytes 2359304 | tf_op jit(solution)/shard_map/ppermute | solution.py:28
  179.4 55.3 %copy-start.8 = (bf16[512,1536]{1,0:T(8,128)(2,1)}, bf16[512,1536]{1,0:T(8,128)(2,1)S(1)}, u32[]{:S(2)}) copy-start(bf16[512,1536]{1,0:T(8,128)(2,1)S(1)} %maximum_select_fusion.1) | copy-start | bytes 4718596
  179.4 55.3 %collective-permute-start.1 = (bf16[512,1536]{1,0:T(8,128)(2,1)S(1)}, bf16[512,1536]{1,0:T(8,128)(2,1)S(1)}, u32[]{:S(2)}, u32[]{:S(2)}) collective-permute-start(bf16[512,1536]{1,0:T(8,128)(2,1)S(1)} %maximum_select_fusion.1), channel_id=1, source_target_pairs={{0,8},{4,12},{8,0},{12,4},{16,24},{20,28},{24,16},{28,20},{1,9},{5... | collective-permute-start | bytes 4718600 | tf_op jit(solution)/shard_map/ppermute | solution.py:22
  180.1 46.6 %collective-permute-start.6 = (bf16[512,64]{0,1:T(8,128)(2,1)S(1)}, bf16[512,64]{0,1:T(8,128)(2,1)S(1)}, u32[]{:S(2)}, u32[]{:S(2)}) collective-permute-start(bf16[512,64]{0,1:T(8,128)(2,1)S(1)} %maximum_select_fusion.7), channel_id=1, source_target_pairs={{0,8},{4,12},{8,0},{12,4},{16,24},{20,28},{24,16},{28,20},{1,9},{5... | collective-permute-start | bytes 196616 | tf_op jit(solution)/shard_map/ppermute | solution.py:22
  227.4 29.1 %collective-permute-start.7 = (bf16[768,64]{0,1:T(8,128)(2,1)}, bf16[768,64]{0,1:T(8,128)(2,1)}, u32[]{:S(2)}, u32[]{:S(2)}) collective-permute-start(bf16[768,64]{0,1:T(8,128)(2,1)} %slice.119), channel_id=1, source_target_pairs={{0,16},{4,20},{8,24},{12,28},{1,17},{5,21},{9,25},{13,29},{2,18},{... | collective-permute-start | bytes 294920 | tf_op jit(solution)/shard_map/ppermute | solution.py:28
  234.7 3.9 %copy-start.19 = (bf16[512,1536]{1,0:T(8,128)(2,1)}, bf16[512,1536]{1,0:T(8,128)(2,1)S(1)}, u32[]{:S(2)}) copy-start(bf16[512,1536]{1,0:T(8,128)(2,1)S(1)} %collective-permute-done.1) | copy-start | bytes 4718596
  246.8 1.6 copy-start.2
  248.4 1.6 copy-start.1
  250.0 1.6 copy-start
  256.5 3.1 %copy-start.11 = (pred[256,1024]{1,0:T(8,128)(4,1)S(1)}, pred[256,1024]{1,0:T(8,128)(4,1)}, u32[]{:S(2)}) copy-start(pred[256,1024]{1,0:T(8,128)(4,1)} %get-tuple-element.29) | copy-start | bytes 786436
  259.6 2.9 copy-start.12
  262.5 33.2 %copy-start.7 = (bf16[64,4096]{1,0:T(8,128)(2,1)S(1)}, bf16[64,4096]{1,0:T(8,128)(2,1)}, u32[]{:S(2)}) copy-start(bf16[64,4096]{1,0:T(8,128)(2,1)} %param.14) | copy-start | bytes 1572868
  262.5 34.1 %copy-start.4 = (bf16[192,4096]{1,0:T(8,128)(2,1)S(1)}, bf16[192,4096]{1,0:T(8,128)(2,1)}, u32[]{:S(2)}) copy-start(bf16[192,4096]{1,0:T(8,128)(2,1)} %param.12) | copy-start | bytes 4718596
  265.7 32.6 %copy-start.6 = (bf16[192,2048]{1,0:T(8,128)(2,1)S(1)}, bf16[192,2048]{1,0:T(8,128)(2,1)}, u32[]{:S(2)}) copy-start(bf16[192,2048]{1,0:T(8,128)(2,1)} %param.13) | copy-start | bytes 2359300
  265.7 5.3 %collective-permute-start.8 = (f32[1,4,8,256]{3,2,0,1:T(8,128)S(1)}, f32[1,4,8,256]{3,2,0,1:T(8,128)S(1)}, u32[]{:S(2)}, u32[]{:S(2)}) collective-permute-start(f32[1,4,8,256]{3,2,0,1:T(8,128)S(1)} %maximum_bitcast_fusion), channel_id=1, source_target_pairs={{0,4},{4,0},{8,12},{12,8},{16,20},{20,16},{24,28},{28,24},{1,5},{5... | collective-permute-start | bytes 98312 | tf_op jit(solution)/shard_map/ppermute | solution.py:22
  271.0 4.8 %collective-permute-start.9 = (f32[2,4,8,256]{3,2,0,1:T(8,128)S(1)}, f32[2,4,8,256]{3,2,0,1:T(8,128)S(1)}, u32[]{:S(2)}, u32[]{:S(2)}) collective-permute-start(f32[2,4,8,256]{3,2,0,1:T(8,128)S(1)} %maximum_select_fusion.8), channel_id=1, source_target_pairs={{0,8},{4,12},{8,0},{12,4},{16,24},{20,28},{24,16},{28,20},{1,9},{5... | collective-permute-start | bytes 196616 | tf_op jit(solution)/shard_map/ppermute | solution.py:22
  295.6 3.6 %copy-start.18 = (f32[32]{0:T(128)}, f32[32]{0:T(128)S(1)}, u32[]{:S(2)}) copy-start(f32[32]{0:T(128)S(1)} %pmax.7) | copy-start | bytes 388
  (1 other events, 1.3 us)
where the time goes:
time: 300 us; the launch traced here: 299 us
  waiting for transfers between devices  114 us (38%)
  blocking collectives  83.7 us (28%)
  starting transfers between devices  46.2 us (15%)
  matrix products  29.9 us (10%)
  local copies, waits for them, and re-layouts  16 us (5%)
  other arithmetic  7.27 us (2%)
    ppermute x8, waiting for transfers between devices, from_partner(): return lax.ppermute(value, axis, pairs)  54.5 us
    all_gather x1, blocking collectives, body(): all_segs = lax.all_gather(segment_ids, 'seq', axis=0, tiled=True)  50.2 us
    all_to_all x1, waiting for transfers between devices, body(): lax.all_to_all(sent[1], 'seq', split_axis=0, concat_axis=1, tiled=True)  34.9 us
    all_to_all x1, waiting for transfers between devices, body(): lax.all_to_all(sent[2], 'seq', split_axis=0, concat_axis=1, tiled=True)  25 us
    ppermute x8, starting transfers between devices, from_partner(): return lax.ppermute(value, axis, pairs)  23.1 us
    pmax x1, blocking collectives, body(): head_max = lax.pmax(local_heads, 'seq')  19.1 us
    dot_general x4, matrix products, score_max(): jnp.einsum('qhd,kd->hqk', query_rope, key_rope, preferred_element_type=jn...  11.2 us
    all_gather x1, blocking collectives, body(): lax.all_gather(q_latent, 'head', axis=1, tiled=True)  8.59 us
  transfers between devices with their start and end apart: 13, of which 6 were waited for; matrix products, arithmetic and copies ran while one was open for 10% of the time, Pallas kernels for 0%

commit v1 on v0

--- a/solution.py
+++ b/solution.py
@@ -1,8 +1,11 @@
+import functools
 import math
 
 import jax
 import jax.numpy as jnp
 from jax import lax
+from jax.experimental import pallas as pl
+from jax.experimental.pallas import tpu as pltpu
 from jax.sharding import PartitionSpec as P
 
 D_NOPE = 128
@@ -44,7 +47,7 @@
     return jnp.tile(pieces, (copies, 1, 1))
 
 
-def body(q_latent, kv_latent, k_rope, segment_ids, w_q_nope, w_q_rope, w_kv_nope, threshold):
+def grouped_body(q_latent, kv_latent, k_rope, segment_ids, w_q_nope, w_q_rope, w_kv_nope, threshold):
     q_whole, kv_whole = (
         lax.all_gather(q_latent, "head", axis=1, tiled=True),
         lax.all_gather(kv_latent, "head", axis=1, tiled=True),
@@ -142,6 +145,10 @@
     row_max = own.reshape(heads, rows).T
     local_heads = jnp.max(row_max, axis=0)
     head_max = lax.pmax(local_heads, "seq")
+    return finish(threshold, head_max, row_max, w_q_nope, w_q_rope, w_kv_nope)
+
+
+def finish(threshold, head_max, row_max, w_q_nope, w_q_rope, w_kv_nope):
     clip = threshold[0] / jnp.maximum(head_max, threshold[0])
     root = jnp.sqrt(clip)
     new_q_nope = (w_q_nope.astype(jnp.float32) * jnp.repeat(root, D_NOPE)[None, :]).astype(
@@ -154,6 +161,327 @@
         jnp.bfloat16
     )
     return (new_q_nope, new_q_rope, new_kv_nope, head_max, row_max)
+
+
+MESH = pl.DeviceIdType.MESH
+LANES = 128
+
+
+def other(index, stride):
+    return index + stride - 2 * stride * (index // stride % 2)
+
+
+def gather_kernel(
+    n, m, lat, rope, segs, w_nope, w_rope, w_kv,
+    lat_all, rope_all, segs_all, q_cols, kv_cols,
+    own_q, own_kv, lat_send, lat_recv, rope_send, rope_recv, seg_send, seg_recv,
+    w_send, w_recv, local,
+):
+    s = lax.axis_index("seq")
+    h = lax.axis_index("head")
+    rows, width = lat.shape
+    part = rope.shape[0]
+    nope_cols = w_nope.shape[1] // n
+    rope_cols = w_rope.shape[1] // n
+    kv_width = w_kv.shape[1] // n
+    q_rows = w_nope.shape[0]
+    kv_rows = w_kv.shape[0]
+
+    strides = []
+    stride = m // 2
+    while stride >= 1:
+        strides.append(stride)
+        stride //= 2
+
+    barrier = pltpu.get_barrier_semaphore()
+    for k in range(1, n):
+        pl.semaphore_signal(barrier, inc=1, device_id=(lax.rem(s + k, n), h), device_id_type=MESH)
+    for stride in strides:
+        pl.semaphore_signal(barrier, inc=1, device_id=(s, other(h, stride)), device_id_type=MESH)
+
+    mine_nope = pl.ds(pl.multiple_of(s * nope_cols, LANES), nope_cols)
+    mine_rope = pl.ds(pl.multiple_of(s * rope_cols, LANES), rope_cols)
+    mine_kv = pl.ds(pl.multiple_of(s * kv_width, LANES), kv_width)
+    loads = [
+        pltpu.make_async_copy(w_nope.at[:, mine_nope], own_q.at[:, pl.ds(0, nope_cols)], local.at[0]),
+        pltpu.make_async_copy(w_rope.at[:, mine_rope], own_q.at[:, pl.ds(nope_cols, rope_cols)], local.at[1]),
+        pltpu.make_async_copy(w_kv.at[:, mine_kv], own_kv, local.at[2]),
+    ]
+    for copy in loads:
+        copy.start()
+
+    def lat_at(ps, ph):
+        return lat_all.at[pl.ds(pl.multiple_of(ps * rows, rows), rows), pl.ds(pl.multiple_of(ph * width, LANES), width)]
+
+    def rope_at(ps, ph):
+        return rope_all.at[pl.ds(pl.multiple_of((ps * m + ph) * part, part), part), :]
+
+    stores = [
+        pltpu.make_async_copy(lat, lat_at(s, h), local.at[3]),
+        pltpu.make_async_copy(rope, rope_at(s, h), local.at[4]),
+        pltpu.make_async_copy(segs, segs_all.at[s], local.at[5]),
+    ]
+    for copy in stores:
+        copy.start()
+    pl.semaphore_wait(barrier, n - 1 + len(strides))
+
+    sends = []
+
+    def piece(ps, ph, target, own):
+        slot = len(sends)
+        a = pltpu.make_async_remote_copy(
+            src_ref=lat if own else lat_at(ps, ph), dst_ref=lat_at(ps, ph),
+            send_sem=lat_send.at[slot], recv_sem=lat_recv.at[ps * m + ph],
+            device_id=target, device_id_type=MESH)
+        b = pltpu.make_async_remote_copy(
+            src_ref=rope if own else rope_at(ps, ph), dst_ref=rope_at(ps, ph),
+            send_sem=rope_send.at[slot], recv_sem=rope_recv.at[ps * m + ph],
+            device_id=target, device_id_type=MESH)
+        a.start()
+        b.start()
+        sends.append((a, b))
+
+    def arrive(ps, ph):
+        pltpu.make_async_copy(lat_at(ps, ph), lat_at(ps, ph), lat_recv.at[ps * m + ph]).wait()
+        pltpu.make_async_copy(rope_at(ps, ph), rope_at(ps, ph), rope_recv.at[ps * m + ph]).wait()
+
+    others = []
+
+    def weights(k):
+        p = lax.rem(s + k, n)
+        to = (p, h)
+        q_at = pl.ds(pl.multiple_of(s * q_rows, q_rows), q_rows)
+        kv_at = pl.ds(pl.multiple_of(s * kv_rows, kv_rows), kv_rows)
+        pairs = (
+            (w_nope.at[:, pl.ds(pl.multiple_of(p * nope_cols, LANES), nope_cols)], q_cols.at[q_at, pl.ds(0, nope_cols)]),
+            (w_rope.at[:, pl.ds(pl.multiple_of(p * rope_cols, LANES), rope_cols)], q_cols.at[q_at, pl.ds(nope_cols, rope_cols)]),
+            (w_kv.at[:, pl.ds(pl.multiple_of(p * kv_width, LANES), kv_width)], kv_cols.at[kv_at, :]),
+        )
+        for i, (src, dst) in enumerate(pairs):
+            copy = pltpu.make_async_remote_copy(
+                src_ref=src, dst_ref=dst, send_sem=w_send.at[i * n + k], recv_sem=w_recv.at[i * n + k],
+                device_id=to, device_id_type=MESH)
+            copy.start()
+            others.append(copy)
+
+    pair = other(s, 1)
+    even = list(range(2, n, 2))
+    for k in even:
+        piece(s, h, (lax.rem(s + k, n), h), True)
+    piece(s, h, (pair, h), True)
+    for stride in strides:
+        piece(s, h, (s, other(h, stride)), True)
+    for k in range(1, n):
+        copy = pltpu.make_async_remote_copy(
+            src_ref=segs, dst_ref=segs_all.at[s], send_sem=seg_send.at[k], recv_sem=seg_recv.at[k],
+            device_id=(lax.rem(s + k, n), h), device_id_type=MESH)
+        copy.start()
+        others.append(copy)
+    for k in even:
+        weights(k)
+    for k in even:
+        ps = lax.rem(s + n - k, n)
+        arrive(ps, h)
+        piece(ps, h, (pair, h), False)
+        for stride in strides:
+            piece(ps, h, (s, other(h, stride)), False)
+    for k in range(1, n, 2):
+        weights(k)
+    for copy in loads:
+        copy.wait()
+    keep = [
+        pltpu.make_async_copy(own_q, q_cols.at[pl.ds(pl.multiple_of(s * q_rows, q_rows), q_rows), :], local.at[6]),
+        pltpu.make_async_copy(own_kv, kv_cols.at[pl.ds(pl.multiple_of(s * kv_rows, kv_rows), kv_rows), :], local.at[7]),
+    ]
+    for copy in keep:
+        copy.start()
+    for k in [0] + even:
+        ps = lax.rem(pair + n - k, n)
+        arrive(ps, h)
+        for stride in strides:
+            piece(ps, h, (s, other(h, stride)), False)
+    held = [h]
+    for i, stride in enumerate(strides):
+        fresh = [other(ph, stride) for ph in held]
+        for first in range(n):
+            ps = lax.rem(s + first, n)
+            for ph in fresh:
+                arrive(ps, ph)
+                for later in strides[i + 1:]:
+                    piece(ps, ph, (s, other(h, later)), False)
+        held = held + fresh
+    for copy in others:
+        copy.wait()
+    for a, b in sends:
+        a.wait_send()
+        b.wait_send()
+    for copy in stores + keep:
+        copy.wait()
+
+
+def gather_all(n, m, lat, rope, segs, w_nope, w_rope, w_kv):
+    rows, width = lat.shape
+    part = rope.shape[0]
+    q_width = (w_nope.shape[1] + w_rope.shape[1]) // n
+    kv_width = w_kv.shape[1] // n
+    moves = n // 2 - 1 + n * m
+    any_ref = pl.BlockSpec(memory_space=pl.ANY)
+    vmem = pl.BlockSpec(memory_space=pltpu.VMEM)
+    dma = pltpu.SemaphoreType.DMA
+    return pl.pallas_call(
+        functools.partial(gather_kernel, n, m),
+        out_shape=(
+            jax.ShapeDtypeStruct((n * rows, m * width), lat.dtype),
+            jax.ShapeDtypeStruct((n * m * part, LANES), rope.dtype),
+            jax.ShapeDtypeStruct((n,) + segs.shape, segs.dtype),
+            jax.ShapeDtypeStruct((n * w_nope.shape[0], q_width), w_nope.dtype),
+            jax.ShapeDtypeStruct((n * w_kv.shape[0], kv_width), w_kv.dtype),
+        ),
+        in_specs=[vmem, vmem, vmem, any_ref, any_ref, any_ref],
+        out_specs=(any_ref,) * 5,
+        scratch_shapes=[
+            pltpu.VMEM((w_nope.shape[0], q_width), w_nope.dtype),
+            pltpu.VMEM((w_kv.shape[0], kv_width), w_kv.dtype),
+            dma((moves,)), dma((n * m,)), dma((moves,)), dma((n * m,)), dma((n,)), dma((n,)),
+            dma((3 * n,)), dma((3 * n,)), dma((8,)),
+        ],
+        compiler_params=pltpu.CompilerParams(collective_id=0, has_side_effects=True),
+        name="gather_all",
+    )(lat, rope, segs, w_nope, w_rope, w_kv)
+
+
+def logit_kernel(m, own, q_width, lat, rope, segs, w_q, w_kv, out, keys, seg_cols):
+    block = pl.program_id(0)
+    rows = lat.shape[0]
+    width = lat.shape[1] // m
+    window = (REACH + 1) * rows
+    q_lat = jnp.concatenate([lat[:, i * width : i * width + q_width] for i in range(m)], 1)
+    kv_lat = jnp.concatenate([lat[:, i * width + q_width : (i + 1) * width] for i in range(m)], 1)
+    q_scale = 1.0 / math.sqrt(QLORA)
+    k_scale = 1.0 / math.sqrt(KVLORA)
+    key = (jnp.dot(kv_lat, w_kv[...], preferred_element_type=jnp.float32) * k_scale).astype(jnp.bfloat16)
+    query = (jnp.dot(q_lat, w_q[...], preferred_element_type=jnp.float32) * q_scale).astype(jnp.bfloat16)
+    here = pl.ds(pl.multiple_of(block * rows, rows), rows)
+    lane = lax.broadcasted_iota(jnp.int32, (rows, LANES), 1)
+    twice = rope[...]
+    sides = [
+        jnp.where(lane // D_ROPE == side, twice, jnp.zeros_like(twice)) for side in range(LANES // D_ROPE)
+    ]
+    for i in range(own):
+        keys[i, here, :] = jnp.concatenate(
+            [key[:, i * D_NOPE : (i + 1) * D_NOPE], sides[i % len(sides)]], 1
+        )
+    seg_row = segs[0, 0:1, :]
+    seg_cols[here, :] = jnp.transpose(jnp.broadcast_to(seg_row, (LANES, rows)))
+    start = jnp.maximum(block - REACH, 0) * rows
+    range_keys = pl.ds(pl.multiple_of(start, rows), window)
+    key_segs = seg_cols[range_keys, :]
+    key_segs = jnp.concatenate([key_segs] * (rows // LANES), 1)
+    key_pos = start + lax.broadcasted_iota(jnp.int32, (window, rows), 0)
+    query_pos = block * rows + lax.broadcasted_iota(jnp.int32, (window, rows), 1)
+    allowed = (key_segs == seg_row) & (key_pos <= query_pos)
+    base = own * D_NOPE
+    found = []
+    for i in range(own):
+        pair = base + i // len(sides) * LANES
+        q_head = jnp.concatenate(
+            [query[:, i * D_NOPE : (i + 1) * D_NOPE], query[:, pair : pair + LANES]], 1
+        )
+        logits = lax.dot_general(
+            keys[i, range_keys, :], q_head, (((1,), (1,)), ((), ())), preferred_element_type=jnp.float32
+        )
+        logits = jnp.where(allowed, logits, jnp.float32(-1e30))
+        found.append(jnp.max(logits, axis=0, keepdims=True))
+    out[0:own, here] = jnp.concatenate(found, 0) * (1.0 / math.sqrt(D_NOPE + D_ROPE))
+
+    @pl.when(block == pl.num_programs(0) - 1)
+    def _():
+        top = jnp.max(out[0:own, :], axis=1, keepdims=True)
+        out[own : 2 * own, :] = jnp.broadcast_to(top, (own, out.shape[1]))
+
+
+def logit_maxima(n, m, own, q_width, lat, rope, segs, w_q, w_kv):
+    rows = lat.shape[0] // n
+    return pl.pallas_call(
+        functools.partial(logit_kernel, m, own, q_width),
+        grid=(n,),
+        out_shape=jax.ShapeDtypeStruct((2 * own, lat.shape[0]), jnp.float32),
+        in_specs=[
+            pl.BlockSpec((rows, lat.shape[1]), lambda i: (i, 0)),
+            pl.BlockSpec((rows, LANES), lambda i: (i, 0)),
+            pl.BlockSpec((1,) + segs.shape[1:], lambda i: (i, 0, 0)),
+            pl.BlockSpec(w_q.shape, lambda i: (0, 0)),
+            pl.BlockSpec(w_kv.shape, lambda i: (0, 0)),
+        ],
+        out_specs=pl.BlockSpec((2 * own, lat.shape[0]), lambda i: (0, 0)),
+        scratch_shapes=[
+            pltpu.VMEM((own, lat.shape[0], D_NOPE + LANES), jnp.bfloat16),
+            pltpu.VMEM((lat.shape[0], LANES), jnp.int32),
+        ],
+        compiler_params=pltpu.CompilerParams(dimension_semantics=("arbitrary",)),
+        name="logit_maxima",
+    )(lat, rope, segs, w_q, w_kv)
+
+
+def exchange_kernel(n, maxima, out, send, recv):
+    s = lax.axis_index("seq")
+    h = lax.axis_index("head")
+    rows = out.shape[2]
+    barrier = pltpu.get_barrier_semaphore()
+    for k in range(1, n):
+        pl.semaphore_signal(barrier, inc=1, device_id=(lax.rem(s + k, n), h), device_id_type=MESH)
+    pl.semaphore_wait(barrier, n - 1)
+    copies = []
+    for k in range(1, n):
+        p = lax.rem(s + k, n)
+        copy = pltpu.make_async_remote_copy(
+            src_ref=maxima.at[:, pl.ds(pl.multiple_of(p * rows, rows), rows)], dst_ref=out.at[s],
+            send_sem=send.at[k], recv_sem=recv.at[k], device_id=(p, h), device_id_type=MESH)
+        copy.start()
+        copies.append(copy)
+    out[s] = maxima[:, pl.ds(pl.multiple_of(s * rows, rows), rows)]
+    for copy in copies:
+        copy.wait()
+
+
+def exchange(n, maxima):
+    vmem = pl.BlockSpec(memory_space=pltpu.VMEM)
+    return pl.pallas_call(
+        functools.partial(exchange_kernel, n),
+        out_shape=jax.ShapeDtypeStruct((n, maxima.shape[0], maxima.shape[1] // n), jnp.float32),
+        in_specs=[vmem],
+        out_specs=vmem,
+        scratch_shapes=[pltpu.SemaphoreType.DMA((n,)), pltpu.SemaphoreType.DMA((n,))],
+        compiler_params=pltpu.CompilerParams(collective_id=1, has_side_effects=True),
+        name="exchange",
+    )(maxima)
+
+
+def owned_body(n, m, q_latent, kv_latent, k_rope, segment_ids, w_q_nope, w_q_rope, w_kv_nope, threshold):
+    rows, q_width = q_latent.shape
+    heads = w_q_nope.shape[1] // D_NOPE
+    own = heads // n
+    lat = jnp.concatenate([q_latent, kv_latent], 1)
+    part = rows // m
+    rope = lax.dynamic_slice_in_dim(k_rope, lax.axis_index("head") * part, part, 0)
+    rope = jnp.concatenate([rope] * (LANES // D_ROPE), 1)
+    segs = jnp.broadcast_to(segment_ids[None], (8, rows))
+    lat_all, rope_all, segs_all, w_q, w_kv = gather_all(n, m, lat, rope, segs, w_q_nope, w_q_rope, w_kv_nope)
+    maxima = logit_maxima(n, m, own, q_width, lat_all, rope_all, segs_all, w_q, w_kv)
+    got = exchange(n, maxima)
+    row_max = got[:, :own, :].reshape(heads, rows).T
+    head_max = got[:, own:, 0].reshape(heads)
+    return finish(threshold, head_max, row_max, w_q_nope, w_q_rope, w_kv_nope)
+
+
+def body(n, m, *operands):
+    heads = operands[4].shape[1] // D_NOPE
+    rows = operands[0].shape[0]
+    shares = heads % n == 0 and heads // n % (LANES // D_ROPE) == 0
+    fits = n % 2 == 0 and n > REACH and m & (m - 1) == 0 and rows % LANES == 0 and rows // m % 16 == 0
+    if shares and fits and heads // n % 4 == 0:
+        return owned_body(n, m, *operands)
+    return grouped_body(*operands)
 
 
 def solution(mesh):
@@ -168,4 +496,4 @@
         P(),
     )
     out_specs = (P("seq", "head"), P("seq", "head"), P("seq", "head"), P("head"), P("seq", "head"))
-    return jax.shard_map(body, mesh=mesh, in_specs=in_specs, out_specs=out_specs, check_vma=False)
+    return jax.shard_map(functools.partial(body, mesh.shape["seq"], mesh.shape["head"]), mesh=mesh, in_specs=in_specs, out_specs=out_specs, check_vma=False)

time: 300 us -> 137 us (0.46)
  Pallas kernels: 0 us -> 125 us
  waiting for transfers between devices: 114 us -> 0 us
  blocking collectives: 83.7 us -> 0 us
  starting transfers between devices: 46.2 us -> 0 us
  matrix products: 29.9 us -> 0 us
  local copies, waits for them, and re-layouts: 16 us -> 3.99 us
    pallas_call x0 -> x3, Pallas kernels: none -> 125 us  [the longest x1 90.5 us: gather_all(): pl.pallas_call(functools.partial(gather_kernel, n, m), out_shape=(jax.Sha...]
    all_gather x3 -> x0, blocking collectives: 64.6 us -> none  [the longest x1 50.2 us: body(): all_segs = lax.all_gather(segment_ids, 'seq', axis=0, tiled=True)]
    all_to_all x3 -> x0, waiting for transfers between devices: 59.9 us -> none  [the longest x1 34.9 us: body(): lax.all_to_all(sent[1], 'seq', split_axis=0, concat_axis=1, tiled=True)]
    ppermute x10 -> x0, waiting for transfers between devices: 54.6 us -> none  [the longest x8 54.5 us: from_partner(): return lax.ppermute(value, axis, pairs)]
    ppermute x10 -> x0, starting transfers between devices: 30 us -> none  [the longest x8 23.1 us: from_partner(): return lax.ppermute(value, axis, pairs)]
    dot_general x11 -> x0, matrix products: 29.9 us -> none  [the longest x4 11.2 us: score_max(): jnp.einsum('qhd,kd->hqk', query_rope, key_rope, preferred_element_type=jn...]
    pmax x1 -> x0, blocking collectives: 19.1 us -> none  [body(): head_max = lax.pmax(local_heads, 'seq')]
    all_to_all x3 -> x0, starting transfers between devices: 16.2 us -> none  [the longest x1 7.28 us: body(): lax.all_to_all(sent[2], 'seq', split_axis=0, concat_axis=1, tiled=True)]
  transfers between devices with their start and end apart: 13 -> 0, of which waited for: 6 -> 0; matrix products, arithmetic and copies ran while one was open for 10% -> 0% of each run, Pallas kernels for 0% -> 0%
where the time goes in v1:
time: 137 us; the launch traced here: 136 us
  Pallas kernels  125 us (91%)
  other arithmetic  5.77 us (4%)
  local copies, waits for them, and re-layouts  3.99 us (3%)
    pallas_call x1, Pallas kernels, gather_all(): pl.pallas_call(functools.partial(gather_kernel, n, m), out_shape=(jax.Sha...  90.5 us
    pallas_call x1, Pallas kernels, logit_maxima(): pl.pallas_call(functools.partial(logit_kernel, m, own, q_width), grid=(n,...  20.7 us
    pallas_call x1, Pallas kernels, exchange(): pl.pallas_call(functools.partial(exchange_kernel, n), out_shape=jax.Shape...  14 us

profile of v1, /device:TPU:0, one launch (start us, length us, event | category | flops | bytes accessed | tf_op | source)
XLA Modules:
  0.0 136.3 jit_solution(18231740691236114566)
XLA Ops:
  0.6 0.0 copy-start
  0.7 0.7 copy-done
  1.4 0.1 constant_dynamic-slice_fusion
  1.5 0.1 copy.15
  1.6 0.7 pad_maximum_fusion.1.rope
  2.3 1.7 %pad_maximum_fusion.lat = bf16[256,512]{1,0:T(8,128)(2,1)} fusion(bf16[256,128]{1,0:T(8,128)(2,1)} %param.9, bf16[256,384]{1,0:T(8,128)(2,1)} %param.8), kind=kLoop, calls=%fused_computation.3 | loop fusion | flops 524288 | bytes 524288 | tf_op jit(solution)/shard_map/concatenate | solution.py:464
  4.0 1.3 broadcast_in_dim.6.segs
  5.2 90.5 %gather_all.1 = (bf16[2048,2048]{1,0:T(8,128)(2,1)}, bf16[2048,128]{1,0:T(8,128)(2,1)}, s32[8,8,256]{2,1,0:T(8,128)}, bf16[1536,768]{1,0:T(8,128)(2,1)}, bf16[512,512]{1,0:T(8,128)(2,1)}) custom-call(bf16[256,512]{1,0:T(8,128)(2,1)} %pad_maximum_fusion.lat, bf16[64,128]{1,0:T(8,128)(2,1)} %pad_maximum_fusion.1.rope, s32[8,256]{1,0:T(8,128)} %broadcast_in_dim.6.segs, ...), custom_call_target="tpu_custom_call" | custom-call | tf_op jit(solution)/shard_map/gather_all/pallas_call | solution.py:331
  95.7 0.0 copy-start.1
  95.8 20.7 %logit_maxima.1.maxima = f32[8,2048]{1,0:T(8,128)} custom-call(bf16[2048,2048]{1,0:T(8,128)(2,1)} %get-tuple-element.10.lat, bf16[2048,128]{1,0:T(8,128)(2,1)} %get-tuple-element.11.rope, s32[8,8,256]{2,1,0:T(8,128)} %get-tuple-element.12.segs, bf16[1536,768]{1,0:T(8,128)(2,1)} %get-tuple-element.13.w_q, bf16[512,512]{1,0:T(8,128)(2,1)} %get-tuple-element.14.w_kv), custom_call_target="tpu_custom_call" | custom-call | tf_op jit(solution)/shard_map/logit_maxima/pallas_call | solution.py:405
  116.4 14.0 %exchange.1 = f32[8,8,256]{2,1,0:T(8,128)} custom-call(f32[8,2048]{1,0:T(8,128)} %logit_maxima.1.maxima), custom_call_target="tpu_custom_call" | custom-call | tf_op jit(solution)/shard_map/exchange/pallas_call | solution.py:449
  130.5 0.8 slice_reduce_fusion
  131.3 0.1 reshape_squeeze.3
  131.4 0.0 copy-start.4
  132.1 0.1 broadcast_bitcast_fusion
  132.2 0.0 copy-done.1
  132.2 0.0 copy-start.2
  132.2 1.5 %multiply_convert_fusion = bf16[192,4096]{1,0:T(8,128)(2,1)} fusion(bf16[192,4096]{1,0:T(8,128)(2,1)S(1)} %copy-done.1, f32[4096]{0:T(1024)S(1)} %broadcast_bitcast_fusion), kind=kLoop, calls=%fused_computation | loop fusion | flops 2359296 | bytes 3162112 | tf_op jit(solution)/shard_map/convert_element_type | solution.py:154
  133.6 0.0 copy-done.4
  133.6 0.0 copy-start.3
  133.6 0.0 slice-start
  133.6 0.1 broadcast_in_dim.15
  133.7 0.1 mul.35
  133.8 0.0 copy-done.2
  133.8 1.0 multiply_convert_fusion.1
  134.8 0.0 copy-done.3
  134.8 0.9 multiply_convert_fusion.2
  135.7 0.0 slice-done
  135.7 0.6 reshape.16
  (1 shorter events, 0.0 us)
Async XLA Ops:
  0.6 0.8 copy-start
  95.7 36.4 %copy-start.1 = (bf16[192,4096]{1,0:T(8,128)(2,1)S(1)}, bf16[192,4096]{1,0:T(8,128)(2,1)}, u32[]{:S(2)}) copy-start(bf16[192,4096]{1,0:T(8,128)(2,1)} %w_nope.1) | copy-start | bytes 4718596
  131.4 2.2 %copy-start.4 = (f32[32]{0:T(128)}, f32[32]{0:T(128)S(1)}, u32[]{:S(2)}) copy-start(f32[32]{0:T(128)S(1)} %reshape_squeeze.3) | copy-start | bytes 388
  132.2 1.6 %copy-start.2 = (bf16[192,2048]{1,0:T(8,128)(2,1)S(1)}, bf16[192,2048]{1,0:T(8,128)(2,1)}, u32[]{:S(2)}) copy-start(bf16[192,2048]{1,0:T(8,128)(2,1)} %w_rope.1) | copy-start | bytes 2359300
  133.6 1.2 copy-start.3
  133.6 2.1 %slice-start = ((f32[8,8,256]{2,1,0:T(8,128)}), f32[8,4,256]{2,1,0:T(4,128)S(1)}, s32[]{:S(2)}) async-start(f32[8,8,256]{2,1,0:T(8,128)} %exchange.1), calls=%async_computation | async-start | bytes 65536 | tf_op jit(solution)/shard_map/slice | solution.py:472

commit v2 on v1

--- a/solution.py
+++ b/solution.py
@@ -172,15 +172,15 @@
 
 
 def gather_kernel(
-    n, m, lat, rope, segs, w_nope, w_rope, w_kv,
-    lat_all, rope_all, segs_all, q_cols, kv_cols,
-    own_q, own_kv, lat_send, lat_recv, rope_send, rope_recv, seg_send, seg_recv,
+    n, m, q_lat, kv_lat, rope, segs, w_nope, w_rope, w_kv,
+    q_all, kv_all, rope_all, segs_all, q_cols, kv_cols,
+    own_q, own_kv, q_send, q_recv, kv_send, kv_recv, rope_send, rope_recv, seg_send, seg_recv,
     w_send, w_recv, local,
 ):
     s = lax.axis_index("seq")
     h = lax.axis_index("head")
-    rows, width = lat.shape
-    part = rope.shape[0]
+    rows = q_lat.shape[0]
+    part = rope.shape[0] // m
     nope_cols = w_nope.shape[1] // n
     rope_cols = w_rope.shape[1] // n
     kv_width = w_kv.shape[1] // n
@@ -210,40 +210,52 @@
     for copy in loads:
         copy.start()
 
-    def lat_at(ps, ph):
-        return lat_all.at[pl.ds(pl.multiple_of(ps * rows, rows), rows), pl.ds(pl.multiple_of(ph * width, LANES), width)]
+    def window(whole, lat, ps, ph):
+        width = lat.shape[1]
+        return whole.at[pl.ds(pl.multiple_of(ps * rows, rows), rows), pl.ds(pl.multiple_of(ph * width, LANES), width)]
 
     def rope_at(ps, ph):
-        return rope_all.at[pl.ds(pl.multiple_of((ps * m + ph) * part, part), part), :]
-
+        return rope_all.at[ps, pl.ds(pl.multiple_of(ph * part, part), part), :]
+
+    def places(ps, ph):
+        return window(q_all, q_lat, ps, ph), window(kv_all, kv_lat, ps, ph), rope_at(ps, ph)
+
+    mine = (q_lat, kv_lat, rope.at[pl.ds(pl.multiple_of(h * part, part), part), :])
+    send_sems = (q_send, kv_send, rope_send)
+    recv_sems = (q_recv, kv_recv, rope_recv)
     stores = [
-        pltpu.make_async_copy(lat, lat_at(s, h), local.at[3]),
-        pltpu.make_async_copy(rope, rope_at(s, h), local.at[4]),
-        pltpu.make_async_copy(segs, segs_all.at[s], local.at[5]),
+        pltpu.make_async_copy(src, dst, local.at[3 + i])
+        for i, (src, dst) in enumerate(zip(mine + (segs,), places(s, h) + (segs_all.at[s],)))
     ]
     for copy in stores:
         copy.start()
     pl.semaphore_wait(barrier, n - 1 + len(strides))
 
     sends = []
-
-    def piece(ps, ph, target, own):
-        slot = len(sends)
-        a = pltpu.make_async_remote_copy(
-            src_ref=lat if own else lat_at(ps, ph), dst_ref=lat_at(ps, ph),
-            send_sem=lat_send.at[slot], recv_sem=lat_recv.at[ps * m + ph],
-            device_id=target, device_id_type=MESH)
-        b = pltpu.make_async_remote_copy(
-            src_ref=rope if own else rope_at(ps, ph), dst_ref=rope_at(ps, ph),
-            send_sem=rope_send.at[slot], recv_sem=rope_recv.at[ps * m + ph],
-            device_id=target, device_id_type=MESH)
-        a.start()
-        b.start()
-        sends.append((a, b))
+    slots = [0]
+
+    def piece(ps, ph, target, own, when=None):
+        slot = slots[0]
+        slots[0] += 1
+        copies = [
+            pltpu.make_async_remote_copy(
+                src_ref=src, dst_ref=dst, send_sem=sent.at[slot], recv_sem=got.at[ps * m + ph],
+                device_id=target, device_id_type=MESH)
+            for src, dst, sent, got in zip(
+                mine if own else places(ps, ph), places(ps, ph), send_sems, recv_sems)
+        ]
+        for copy in copies:
+            copy.start()
+
+        def drain():
+            for sent, src in zip(send_sems, mine):
+                pltpu.make_async_copy(src, src, sent.at[slot]).wait()
+
+        sends.append((when, drain))
 
     def arrive(ps, ph):
-        pltpu.make_async_copy(lat_at(ps, ph), lat_at(ps, ph), lat_recv.at[ps * m + ph]).wait()
-        pltpu.make_async_copy(rope_at(ps, ph), rope_at(ps, ph), rope_recv.at[ps * m + ph]).wait()
+        for at, got in zip(places(ps, ph), recv_sems):
+            pltpu.make_async_copy(at, at, got.at[ps * m + ph]).wait()
 
     others = []
 
@@ -266,32 +278,52 @@
 
     pair = other(s, 1)
     even = list(range(2, n, 2))
-    for k in even:
-        piece(s, h, (lax.rem(s + k, n), h), True)
+
+    def inside(index):
+        return (index >= 0) & (index < n)
+
+    for sign in (-2, 2):
+        @pl.when(inside(s + sign))
+        def _(sign=sign):
+            piece(s, h, (s + sign, h), True, lambda: inside(s + sign))
     piece(s, h, (pair, h), True)
     for stride in strides:
         piece(s, h, (s, other(h, stride)), True)
-    for k in range(1, n):
-        copy = pltpu.make_async_remote_copy(
-            src_ref=segs, dst_ref=segs_all.at[s], send_sem=seg_send.at[k], recv_sem=seg_recv.at[k],
-            device_id=(lax.rem(s + k, n), h), device_id_type=MESH)
-        copy.start()
-        others.append(copy)
-    for k in even:
-        weights(k)
-    for k in even:
-        ps = lax.rem(s + n - k, n)
-        arrive(ps, h)
-        piece(ps, h, (pair, h), False)
-        for stride in strides:
-            piece(ps, h, (s, other(h, stride)), False)
+    for step in range(1, n // 2):
+        for sign in (-2, 2):
+            ps = s + sign * step
+            ahead = s - sign
+
+            @pl.when(inside(ps) & inside(ahead))
+            def _(ps=ps, ahead=ahead):
+                arrive(ps, h)
+                piece(ps, h, (ahead, h), False, lambda: inside(ps) & inside(ahead))
+
+            @pl.when(inside(ps) & (ahead < 0) | inside(ps) & (ahead >= n))
+            def _(ps=ps):
+                arrive(ps, h)
+
+            @pl.when(inside(ps))
+            def _(ps=ps):
+                piece(ps, h, (pair, h), False, lambda: inside(ps))
+                for stride in strides:
+                    piece(ps, h, (s, other(h, stride)), False, lambda: inside(ps))
+        if step == 1:
+            for k in range(1, n):
+                copy = pltpu.make_async_remote_copy(
+                    src_ref=segs, dst_ref=segs_all.at[s], send_sem=seg_send.at[k], recv_sem=seg_recv.at[k],
+                    device_id=(lax.rem(s + k, n), h), device_id_type=MESH)
+                copy.start()
+                others.append(copy)
+            for k in even:
+                weights(k)
     for k in range(1, n, 2):
         weights(k)
     for copy in loads:
         copy.wait()
     keep = [
-        pltpu.make_async_copy(own_q, q_cols.at[pl.ds(pl.multiple_of(s * q_rows, q_rows), q_rows), :], local.at[6]),
-        pltpu.make_async_copy(own_kv, kv_cols.at[pl.ds(pl.multiple_of(s * kv_rows, kv_rows), kv_rows), :], local.at[7]),
+        pltpu.make_async_copy(own_q, q_cols.at[pl.ds(pl.multiple_of(s * q_rows, q_rows), q_rows), :], local.at[7]),
+        pltpu.make_async_copy(own_kv, kv_cols.at[pl.ds(pl.multiple_of(s * kv_rows, kv_rows), kv_rows), :], local.at[8]),
     ]
     for copy in keep:
         copy.start()
@@ -312,58 +344,59 @@
         held = held + fresh
     for copy in others:
         copy.wait()
-    for a, b in sends:
-        a.wait_send()
-        b.wait_send()
+    for when, drain in sends:
+        if when is None:
+            drain()
+        else:
+            pl.when(when())(drain)
     for copy in stores + keep:
         copy.wait()
 
 
-def gather_all(n, m, lat, rope, segs, w_nope, w_rope, w_kv):
-    rows, width = lat.shape
-    part = rope.shape[0]
+def gather_all(n, m, q_lat, kv_lat, rope, segs, w_nope, w_rope, w_kv):
+    rows = q_lat.shape[0]
     q_width = (w_nope.shape[1] + w_rope.shape[1]) // n
     kv_width = w_kv.shape[1] // n
-    moves = n // 2 - 1 + n * m
+    moves = 2 + 2 * (n // 2 - 1) + (n - 1) * (m + 1) + n * m
     any_ref = pl.BlockSpec(memory_space=pl.ANY)
     vmem = pl.BlockSpec(memory_space=pltpu.VMEM)
     dma = pltpu.SemaphoreType.DMA
     return pl.pallas_call(
         functools.partial(gather_kernel, n, m),
         out_shape=(
-            jax.ShapeDtypeStruct((n * rows, m * width), lat.dtype),
-            jax.ShapeDtypeStruct((n * m * part, LANES), rope.dtype),
+            jax.ShapeDtypeStruct((n * rows, m * q_lat.shape[1]), q_lat.dtype),
+            jax.ShapeDtypeStruct((n * rows, m * kv_lat.shape[1]), kv_lat.dtype),
+            jax.ShapeDtypeStruct((n,) + rope.shape, rope.dtype),
             jax.ShapeDtypeStruct((n,) + segs.shape, segs.dtype),
             jax.ShapeDtypeStruct((n * w_nope.shape[0], q_width), w_nope.dtype),
             jax.ShapeDtypeStruct((n * w_kv.shape[0], kv_width), w_kv.dtype),
         ),
-        in_specs=[vmem, vmem, vmem, any_ref, any_ref, any_ref],
-        out_specs=(any_ref,) * 5,
+        in_specs=[vmem, vmem, vmem, vmem, any_ref, any_ref, any_ref],
+        out_specs=(any_ref,) * 6,
         scratch_shapes=[
             pltpu.VMEM((w_nope.shape[0], q_width), w_nope.dtype),
             pltpu.VMEM((w_kv.shape[0], kv_width), w_kv.dtype),
-            dma((moves,)), dma((n * m,)), dma((moves,)), dma((n * m,)), dma((n,)), dma((n,)),
-            dma((3 * n,)), dma((3 * n,)), dma((8,)),
+            dma((moves,)), dma((n * m,)), dma((moves,)), dma((n * m,)), dma((moves,)), dma((n * m,)),
+            dma((n,)), dma((n,)),
+            dma((3 * n,)), dma((3 * n,)), dma((9,)),
         ],
         compiler_params=pltpu.CompilerParams(collective_id=0, has_side_effects=True),
         name="gather_all",
-    )(lat, rope, segs, w_nope, w_rope, w_kv)
-
-
-def logit_kernel(m, own, q_width, lat, rope, segs, w_q, w_kv, out, keys, seg_cols):
+    )(q_lat, kv_lat, rope, segs, w_nope, w_rope, w_kv)
+
+
+def logit_kernel(own, q_lat, kv_lat, rope, segs, w_q, w_kv, out, keys, seg_cols):
     block = pl.program_id(0)
-    rows = lat.shape[0]
-    width = lat.shape[1] // m
+    rows = q_lat.shape[0]
     window = (REACH + 1) * rows
-    q_lat = jnp.concatenate([lat[:, i * width : i * width + q_width] for i in range(m)], 1)
-    kv_lat = jnp.concatenate([lat[:, i * width + q_width : (i + 1) * width] for i in range(m)], 1)
     q_scale = 1.0 / math.sqrt(QLORA)
     k_scale = 1.0 / math.sqrt(KVLORA)
-    key = (jnp.dot(kv_lat, w_kv[...], preferred_element_type=jnp.float32) * k_scale).astype(jnp.bfloat16)
-    query = (jnp.dot(q_lat, w_q[...], preferred_element_type=jnp.float32) * q_scale).astype(jnp.bfloat16)
+    key = (jnp.dot(kv_lat[...], w_kv[...], preferred_element_type=jnp.float32) * k_scale).astype(jnp.bfloat16)
+    query = (jnp.dot(q_lat[...], w_q[...], preferred_element_type=jnp.float32) * q_scale).astype(jnp.bfloat16)
     here = pl.ds(pl.multiple_of(block * rows, rows), rows)
     lane = lax.broadcasted_iota(jnp.int32, (rows, LANES), 1)
-    twice = rope[...]
+    turned = jnp.concatenate([rope[0].astype(jnp.float32)] * (LANES // D_ROPE), 0)
+    twice = jnp.transpose(turned).astype(jnp.bfloat16)
     sides = [
         jnp.where(lane // D_ROPE == side, twice, jnp.zeros_like(twice)) for side in range(LANES // D_ROPE)
     ]
@@ -371,7 +404,7 @@
         keys[i, here, :] = jnp.concatenate(
             [key[:, i * D_NOPE : (i + 1) * D_NOPE], sides[i % len(sides)]], 1
         )
-    seg_row = segs[0, 0:1, :]
+    seg_row = segs[0]
     seg_cols[here, :] = jnp.transpose(jnp.broadcast_to(seg_row, (LANES, rows)))
     start = jnp.maximum(block - REACH, 0) * rows
     range_keys = pl.ds(pl.multiple_of(start, rows), window)
@@ -400,27 +433,28 @@
         out[own : 2 * own, :] = jnp.broadcast_to(top, (own, out.shape[1]))
 
 
-def logit_maxima(n, m, own, q_width, lat, rope, segs, w_q, w_kv):
-    rows = lat.shape[0] // n
+def logit_maxima(n, own, q_lat, kv_lat, rope, segs, w_q, w_kv):
+    rows = q_lat.shape[0] // n
     return pl.pallas_call(
-        functools.partial(logit_kernel, m, own, q_width),
+        functools.partial(logit_kernel, own),
         grid=(n,),
-        out_shape=jax.ShapeDtypeStruct((2 * own, lat.shape[0]), jnp.float32),
+        out_shape=jax.ShapeDtypeStruct((2 * own, q_lat.shape[0]), jnp.float32),
         in_specs=[
-            pl.BlockSpec((rows, lat.shape[1]), lambda i: (i, 0)),
-            pl.BlockSpec((rows, LANES), lambda i: (i, 0)),
+            pl.BlockSpec((rows, q_lat.shape[1]), lambda i: (i, 0)),
+            pl.BlockSpec((rows, kv_lat.shape[1]), lambda i: (i, 0)),
+            pl.BlockSpec((1,) + rope.shape[1:], lambda i: (i, 0, 0)),
             pl.BlockSpec((1,) + segs.shape[1:], lambda i: (i, 0, 0)),
             pl.BlockSpec(w_q.shape, lambda i: (0, 0)),
             pl.BlockSpec(w_kv.shape, lambda i: (0, 0)),
         ],
-        out_specs=pl.BlockSpec((2 * own, lat.shape[0]), lambda i: (0, 0)),
+        out_specs=pl.BlockSpec((2 * own, q_lat.shape[0]), lambda i: (0, 0)),
         scratch_shapes=[
-            pltpu.VMEM((own, lat.shape[0], D_NOPE + LANES), jnp.bfloat16),
-            pltpu.VMEM((lat.shape[0], LANES), jnp.int32),
+            pltpu.VMEM((own, q_lat.shape[0], D_NOPE + LANES), jnp.bfloat16),
+            pltpu.VMEM((q_lat.shape[0], LANES), jnp.int32),
         ],
         compiler_params=pltpu.CompilerParams(dimension_semantics=("arbitrary",)),
         name="logit_maxima",
-    )(lat, rope, segs, w_q, w_kv)
+    )(q_lat, kv_lat, rope, segs, w_q, w_kv)
 
 
 def exchange_kernel(n, maxima, out, send, recv):
@@ -458,16 +492,13 @@
 
 
 def owned_body(n, m, q_latent, kv_latent, k_rope, segment_ids, w_q_nope, w_q_rope, w_kv_nope, threshold):
-    rows, q_width = q_latent.shape
+    rows = q_latent.shape[0]
     heads = w_q_nope.shape[1] // D_NOPE
     own = heads // n
-    lat = jnp.concatenate([q_latent, kv_latent], 1)
-    part = rows // m
-    rope = lax.dynamic_slice_in_dim(k_rope, lax.axis_index("head") * part, part, 0)
-    rope = jnp.concatenate([rope] * (LANES // D_ROPE), 1)
-    segs = jnp.broadcast_to(segment_ids[None], (8, rows))
-    lat_all, rope_all, segs_all, w_q, w_kv = gather_all(n, m, lat, rope, segs, w_q_nope, w_q_rope, w_kv_nope)
-    maxima = logit_maxima(n, m, own, q_width, lat_all, rope_all, segs_all, w_q, w_kv)
+    gathered = gather_all(
+        n, m, q_latent, kv_latent, k_rope.T, segment_ids.reshape(1, rows), w_q_nope, w_q_rope, w_kv_nope
+    )
+    maxima = logit_maxima(n, own, *gathered)
     got = exchange(n, maxima)
     row_max = got[:, :own, :].reshape(heads, rows).T
     head_max = got[:, own:, 0].reshape(heads)
@@ -478,7 +509,7 @@
     heads = operands[4].shape[1] // D_NOPE
     rows = operands[0].shape[0]
     shares = heads % n == 0 and heads // n % (LANES // D_ROPE) == 0
-    fits = n % 2 == 0 and n > REACH and m & (m - 1) == 0 and rows % LANES == 0 and rows // m % 16 == 0
+    fits = n % 2 == 0 and n > REACH and m & (m - 1) == 0 and rows % LANES == 0 and operands[2].shape[1] % (16 * m) == 0
     if shares and fits and heads // n % 4 == 0:
         return owned_body(n, m, *operands)
     return grouped_body(*operands)

time: 137 us -> 142 us (1.036)
  Pallas kernels: 125 us -> 136 us
  other arithmetic: 5.77 us -> 3.39 us
  local copies, waits for them, and re-layouts: 3.99 us -> 1.79 us
    pallas_call x1, Pallas kernels: 90.5 us -> 106 us  [gather_all(): pl.pallas_call(functools.partial(gather_kernel, n, m), out_shape=(jax.Sha...]
    pallas_call x1, Pallas kernels: 14 us -> 8.86 us  [exchange(): pl.pallas_call(functools.partial(exchange_kernel, n), out_shape=jax.Shape...]
    concatenate x2 -> x0, other arithmetic: 2.39 us -> none  [the longest x1 1.69 us: owned_body(): lat = jnp.concatenate([q_latent, kv_latent], 1)]
where the time goes in v2:
time: 142 us
  Pallas kernels  136 us (96%)
  other arithmetic  3.39 us (2%)
  local copies, waits for them, and re-layouts  1.79 us (1%)
    pallas_call x1, Pallas kernels, gather_all(): pl.pallas_call(functools.partial(gather_kernel, n, m), out_shape=(jax.Sha...  106 us
    pallas_call x1, Pallas kernels, logit_maxima(): pl.pallas_call(functools.partial(logit_kernel, own), grid=(n,), out_shape...  20.8 us
    pallas_call x1, Pallas kernels, exchange(): pl.pallas_call(functools.partial(exchange_kernel, n), out_shape=jax.Shape...  8.86 us

profile of v2, /device:TPU:0, one launch (start us, length us, event | category | flops | bytes accessed | tf_op | source)
XLA Modules:
  0.0 142.2 jit_solution(10594723137001362596)
XLA Ops:
  0.6 106.0 %gather_all.1 = (bf16[2048,1536]{1,0:T(8,128)(2,1)}, bf16[2048,512]{1,0:T(8,128)(2,1)}, bf16[8,64,256]{2,1,0:T(8,128)(2,1)}, s32[8,1,256]{2,1,0:T(1,128)}, bf16[...) custom-call(bf16[256,384]{1,0:T(8,128)(2,1)} %q_lat.1, bf16[256,128]{1,0:T(8,128)(2,1)} %kv_lat.1, ...), custom_call_target="tpu_custom_call" | custom-call | tf_op jit(solution)/shard_map/gather_all/pallas_call | solution.py:364
  106.7 0.0 copy-start
  106.7 20.8 %logit_maxima.1.maxima = f32[8,2048]{1,0:T(8,128)} custom-call(bf16[2048,1536]{1,0:T(8,128)(2,1)} %get-tuple-element.11.q_lat, bf16[2048,512]{1,0:T(8,128)(2,1)} %get-tuple-element.12.kv_lat, bf16[8,64,256]{2,1,0:T(8,128)(2,1)} %get-tuple-element.13.rope, s32[8,1,256]{2,1,0:T(1,128)} %get-tuple-element.14.segs, bf16[1536,768]{1,0:T(8,128)(2,1)} %get-tuple-element.15.w_q, ...), custom_call_target="tpu_custom_call" | custom-call | tf_op jit(solution)/shard_map/logit_maxima/pallas_call | solution.py:438
  127.5 8.9 %exchange.1 = f32[8,8,256]{2,1,0:T(8,128)} custom-call(f32[8,2048]{1,0:T(8,128)} %logit_maxima.1.maxima), custom_call_target="tpu_custom_call" | custom-call | tf_op jit(solution)/shard_map/exchange/pallas_call | solution.py:483
  136.4 0.8 slice_reduce_fusion
  137.2 0.1 reshape_squeeze.3
  137.3 0.0 copy-start.3
  138.0 0.1 broadcast_bitcast_fusion
  138.0 0.0 copy-done
  138.0 0.0 copy-start.2
  138.0 0.0 copy-start.1
  138.0 1.5 %multiply_convert_fusion = bf16[192,4096]{1,0:T(8,128)(2,1)} fusion(bf16[192,4096]{1,0:T(8,128)(2,1)S(1)} %copy-done, f32[4096]{0:T(1024)S(1)} %broadcast_bitcast_fusion), kind=kLoop, calls=%fused_computation | loop fusion | flops 2359296 | bytes 3162112 | tf_op jit(solution)/shard_map/convert_element_type | solution.py:154
  139.5 0.0 copy-done.3
  139.5 0.0 copy-done.2
  139.5 0.0 slice-start
  139.5 0.9 multiply_convert_fusion.2
  140.4 0.1 broadcast_in_dim.8
  140.5 0.1 mul.31
  140.5 0.0 copy-done.1
  140.5 1.0 multiply_convert_fusion.1
  141.6 0.0 slice-done
  141.6 0.6 reshape.19
  (1 shorter events, 0.0 us)
Async XLA Ops:
  106.7 31.3 %copy-start = (bf16[192,4096]{1,0:T(8,128)(2,1)S(1)}, bf16[192,4096]{1,0:T(8,128)(2,1)}, u32[]{:S(2)}) copy-start(bf16[192,4096]{1,0:T(8,128)(2,1)} %w_nope.1) | copy-start | bytes 4718596
  137.3 2.2 %copy-start.3 = (f32[32]{0:T(128)}, f32[32]{0:T(128)S(1)}, u32[]{:S(2)}) copy-start(f32[32]{0:T(128)S(1)} %reshape_squeeze.3) | copy-start | bytes 388
  138.0 1.5 %copy-start.2 = (bf16[64,4096]{1,0:T(8,128)(2,1)S(1)}, bf16[64,4096]{1,0:T(8,128)(2,1)}, u32[]{:S(2)}) copy-start(bf16[64,4096]{1,0:T(8,128)(2,1)} %w_kv.1) | copy-start | bytes 1572868
  138.0 2.5 %copy-start.1 = (bf16[192,2048]{1,0:T(8,128)(2,1)S(1)}, bf16[192,2048]{1,0:T(8,128)(2,1)}, u32[]{:S(2)}) copy-start(bf16[192,2048]{1,0:T(8,128)(2,1)} %w_rope.1) | copy-start | bytes 2359300
  139.5 2.1 %slice-start = ((f32[8,8,256]{2,1,0:T(8,128)}), f32[8,4,256]{2,1,0:T(4,128)S(1)}, s32[]{:S(2)}) async-start(f32[8,8,256]{2,1,0:T(8,128)} %exchange.1), calls=%async_computation | async-start | bytes 65536 | tf_op jit(solution)/shard_map/slice | solution.py:503

commit v3 on v2

--- a/solution.py
+++ b/solution.py
@@ -234,7 +234,7 @@
     sends = []
     slots = [0]
 
-    def piece(ps, ph, target, own, when=None):
+    def piece(ps, ph, target, own):
         slot = slots[0]
         slots[0] += 1
         copies = [
@@ -251,7 +251,7 @@
             for sent, src in zip(send_sems, mine):
                 pltpu.make_async_copy(src, src, sent.at[slot]).wait()
 
-        sends.append((when, drain))
+        sends.append(drain)
 
     def arrive(ps, ph):
         for at, got in zip(places(ps, ph), recv_sems):
@@ -279,44 +279,25 @@
     pair = other(s, 1)
     even = list(range(2, n, 2))
 
-    def inside(index):
-        return (index >= 0) & (index < n)
-
-    for sign in (-2, 2):
-        @pl.when(inside(s + sign))
-        def _(sign=sign):
-            piece(s, h, (s + sign, h), True, lambda: inside(s + sign))
+    for k in even:
+        piece(s, h, (lax.rem(s + k, n), h), True)
     piece(s, h, (pair, h), True)
     for stride in strides:
         piece(s, h, (s, other(h, stride)), True)
-    for step in range(1, n // 2):
-        for sign in (-2, 2):
-            ps = s + sign * step
-            ahead = s - sign
-
-            @pl.when(inside(ps) & inside(ahead))
-            def _(ps=ps, ahead=ahead):
-                arrive(ps, h)
-                piece(ps, h, (ahead, h), False, lambda: inside(ps) & inside(ahead))
-
-            @pl.when(inside(ps) & (ahead < 0) | inside(ps) & (ahead >= n))
-            def _(ps=ps):
-                arrive(ps, h)
-
-            @pl.when(inside(ps))
-            def _(ps=ps):
-                piece(ps, h, (pair, h), False, lambda: inside(ps))
-                for stride in strides:
-                    piece(ps, h, (s, other(h, stride)), False, lambda: inside(ps))
-        if step == 1:
-            for k in range(1, n):
-                copy = pltpu.make_async_remote_copy(
-                    src_ref=segs, dst_ref=segs_all.at[s], send_sem=seg_send.at[k], recv_sem=seg_recv.at[k],
-                    device_id=(lax.rem(s + k, n), h), device_id_type=MESH)
-                copy.start()
-                others.append(copy)
-            for k in even:
-                weights(k)
+    for k in range(1, n):
+        copy = pltpu.make_async_remote_copy(
+            src_ref=segs, dst_ref=segs_all.at[s], send_sem=seg_send.at[k], recv_sem=seg_recv.at[k],
+            device_id=(lax.rem(s + k, n), h), device_id_type=MESH)
+        copy.start()
+        others.append(copy)
+    for k in even:
+        weights(k)
+    for k in even:
+        ps = lax.rem(s + n - k, n)
+        arrive(ps, h)
+        piece(ps, h, (pair, h), False)
+        for stride in strides:
+            piece(ps, h, (s, other(h, stride)), False)
     for k in range(1, n, 2):
         weights(k)
     for copy in loads:
@@ -344,11 +325,8 @@
         held = held + fresh
     for copy in others:
         copy.wait()
-    for when, drain in sends:
-        if when is None:
-            drain()
-        else:
-            pl.when(when())(drain)
+    for drain in sends:
+        drain()
     for copy in stores + keep:
         copy.wait()
 
@@ -357,7 +335,7 @@
     rows = q_lat.shape[0]
     q_width = (w_nope.shape[1] + w_rope.shape[1]) // n
     kv_width = w_kv.shape[1] // n
-    moves = 2 + 2 * (n // 2 - 1) + (n - 1) * (m + 1) + n * m
+    moves = n // 2 - 1 + n * m
     any_ref = pl.BlockSpec(memory_space=pl.ANY)
     vmem = pl.BlockSpec(memory_space=pltpu.VMEM)
     dma = pltpu.SemaphoreType.DMA

time: 142 us -> 131 us (0.923)
  Pallas kernels: 136 us -> 124 us
    pallas_call x1, Pallas kernels: 106 us -> 89.3 us  [gather_all(): pl.pallas_call(functools.partial(gather_kernel, n, m), out_shape=(jax.Sha...]
    pallas_call x1, Pallas kernels: 8.86 us -> 14 us  [exchange(): pl.pallas_call(functools.partial(exchange_kernel, n), out_shape=jax.Shape...]
where the time goes in v3:
time: 131 us
  Pallas kernels  124 us (95%)
  other arithmetic  3.39 us (3%)
  local copies, waits for them, and re-layouts  1.79 us (1%)
  between operations  1.33 us (1%)
    pallas_call x1, Pallas kernels, gather_all(): pl.pallas_call(functools.partial(gather_kernel, n, m), out_shape=(jax.Sha...  89.3 us
    pallas_call x1, Pallas kernels, logit_maxima(): pl.pallas_call(functools.partial(logit_kernel, own), grid=(n,), out_shape...  20.8 us
    pallas_call x1, Pallas kernels, exchange(): pl.pallas_call(functools.partial(exchange_kernel, n), out_shape=jax.Shape...  14 us

profile of v3, /device:TPU:0, one launch (start us, length us, event | category | flops | bytes accessed | tf_op | source)
XLA Modules:
  0.0 130.6 jit_solution(15503148180434036026)
XLA Ops:
  0.6 89.3 %gather_all.1 = (bf16[2048,1536]{1,0:T(8,128)(2,1)}, bf16[2048,512]{1,0:T(8,128)(2,1)}, bf16[8,64,256]{2,1,0:T(8,128)(2,1)}, s32[8,1,256]{2,1,0:T(1,128)}, bf16[...) custom-call(bf16[256,384]{1,0:T(8,128)(2,1)} %q_lat.1, bf16[256,128]{1,0:T(8,128)(2,1)} %kv_lat.1, ...), custom_call_target="tpu_custom_call" | custom-call | tf_op jit(solution)/shard_map/gather_all/pallas_call | solution.py:342
  89.9 0.0 copy-start
  89.9 20.8 %logit_maxima.1.maxima = f32[8,2048]{1,0:T(8,128)} custom-call(bf16[2048,1536]{1,0:T(8,128)(2,1)} %get-tuple-element.11.q_lat, bf16[2048,512]{1,0:T(8,128)(2,1)} %get-tuple-element.12.kv_lat, bf16[8,64,256]{2,1,0:T(8,128)(2,1)} %get-tuple-element.13.rope, s32[8,1,256]{2,1,0:T(1,128)} %get-tuple-element.14.segs, bf16[1536,768]{1,0:T(8,128)(2,1)} %get-tuple-element.15.w_q, ...), custom_call_target="tpu_custom_call" | custom-call | tf_op jit(solution)/shard_map/logit_maxima/pallas_call | solution.py:416
  110.7 14.0 %exchange.1 = f32[8,8,256]{2,1,0:T(8,128)} custom-call(f32[8,2048]{1,0:T(8,128)} %logit_maxima.1.maxima), custom_call_target="tpu_custom_call" | custom-call | tf_op jit(solution)/shard_map/exchange/pallas_call | solution.py:461
  124.8 0.8 slice_reduce_fusion
  125.6 0.1 reshape_squeeze.3
  125.7 0.0 copy-start.3
  126.4 0.1 broadcast_bitcast_fusion
  126.4 0.0 copy-done
  126.4 0.0 copy-start.2
  126.4 0.0 copy-start.1
  126.4 1.5 %multiply_convert_fusion = bf16[192,4096]{1,0:T(8,128)(2,1)} fusion(bf16[192,4096]{1,0:T(8,128)(2,1)S(1)} %copy-done, f32[4096]{0:T(1024)S(1)} %broadcast_bitcast_fusion), kind=kLoop, calls=%fused_computation | loop fusion | flops 2359296 | bytes 3162112 | tf_op jit(solution)/shard_map/convert_element_type | solution.py:154
  127.9 0.0 copy-done.3
  127.9 0.0 copy-done.2
  127.9 0.0 slice-start
  127.9 0.9 multiply_convert_fusion.2
  128.8 0.1 broadcast_in_dim.8
  128.9 0.1 mul.31
  128.9 0.0 copy-done.1
  128.9 1.0 multiply_convert_fusion.1
  130.0 0.0 slice-done
  130.0 0.6 reshape.19
  (1 shorter events, 0.0 us)
Async XLA Ops:
  89.9 36.5 %copy-start = (bf16[192,4096]{1,0:T(8,128)(2,1)S(1)}, bf16[192,4096]{1,0:T(8,128)(2,1)}, u32[]{:S(2)}) copy-start(bf16[192,4096]{1,0:T(8,128)(2,1)} %w_nope.1) | copy-start | bytes 4718596
  125.7 2.2 %copy-start.3 = (f32[32]{0:T(128)}, f32[32]{0:T(128)S(1)}, u32[]{:S(2)}) copy-start(f32[32]{0:T(128)S(1)} %reshape_squeeze.3) | copy-start | bytes 388
  126.4 1.5 %copy-start.2 = (bf16[64,4096]{1,0:T(8,128)(2,1)S(1)}, bf16[64,4096]{1,0:T(8,128)(2,1)}, u32[]{:S(2)}) copy-start(bf16[64,4096]{1,0:T(8,128)(2,1)} %w_kv.1) | copy-start | bytes 1572868
  126.4 2.5 %copy-start.1 = (bf16[192,2048]{1,0:T(8,128)(2,1)S(1)}, bf16[192,2048]{1,0:T(8,128)(2,1)}, u32[]{:S(2)}) copy-start(bf16[192,2048]{1,0:T(8,128)(2,1)} %w_rope.1) | copy-start | bytes 2359300
  127.9 2.1 %slice-start = ((f32[8,8,256]{2,1,0:T(8,128)}), f32[8,4,256]{2,1,0:T(4,128)S(1)}, s32[]{:S(2)}) async-start(f32[8,8,256]{2,1,0:T(8,128)} %exchange.1), calls=%async_computation | async-start | bytes 65536 | tf_op jit(solution)/shard_map/slice | solution.py:481
